TPU v7x, 256 devices: a whole 4x4x8 slice. The times are simulated.
256 devices in a mesh: section: 8 (over x, core), dp: 32 (over z, y).
Axes of the slice: x: 4, y: 4, z: 8, core: 2. Of those that a mesh axis runs over, the one named last changes fastest.
Arguments:
- hidden_in: bfloat16 [8, 2048, 2048], P(None, 'dp'), may hold values from -8 to 8
- norm_gain: bfloat16 [8, 2048], P('section'), may hold values from 0.099609375 to 1.8984375
- router_weight: bfloat16 [8, 2048, 60], P('section'), may hold values from -1 to 1
- expert_scale: bfloat16 [8, 60, 2048], P('section'), may hold values from 1 to 16
- mix_weight: bfloat16 [8, 2048, 2048], P('section'), may hold values from -0.125 to 0.125
- routes: int32 [8, 8, 2048, 4], P('section', None, 'dp'), may hold values from 0 to 59, as said below
Outputs:
- hidden_out: bfloat16 [8, 2048, 2048], P('section', 'dp')
- balance_loss: float32 [8], P('section')
Inputs may be any that keep to these rules, and one draw needn't show every extreme that they name: `routes`: the 4 ids of a token in a layer are distinct.
All inputs are finite; a program needn't handle non-finite values.
Results may differ from a plain program's by a relative error of at most 0.01.
The roundings to bfloat16 on the way count: a program that leaves them out, or rounds other values in their place, can miss the bound.
Values may be sent and summed in bfloat16 or wider, within the bound.
No kernel may reach another device: no remote copies, remote signals or barrier semaphores. Data moves between devices by JAX's collectives and lax.ppermute only.
A program may use at most 64 MiB of HBM per device.

v0:
```python
import functools

import jax
import jax.numpy as jnp
from jax import lax
from jax.experimental import pallas as pl
from jax.experimental.pallas import tpu as pltpu
from jax.sharding import Mesh
from jax.sharding import PartitionSpec as P


SEC = ("x", "c")
CHIPS = 4
CHUNKS = 4
STEPS = 12
COLS = 256
WIDE = 512
VMEM_LIMIT = 12 * 1024 * 1024


def front(rows, load_x, load_gain, load_router, load_scale, ids, nrm, nbf, mixed):
    width = nrm.shape[1]
    acc = None
    for c in range(0, width, COLS):
        xs = load_x(c, COLS).astype(jnp.float32)
        acc = xs * xs if acc is None else acc + xs * xs
    mean_square = jnp.sum(acc, axis=-1, keepdims=True) * jnp.float32(1.0 / width)
    inv = lax.rsqrt(mean_square + 1e-06)
    for c in range(0, width, COLS):
        xs = load_x(c, COLS).astype(jnp.float32)
        normed = xs * inv * load_gain(c, COLS).astype(jnp.float32)
        nrm[0:rows, c : c + COLS] = normed
        nbf[0:rows, c : c + COLS] = normed.astype(jnp.bfloat16)
    logits = lax.dot_general(
        load_router(),
        nbf[0:rows, :],
        (((1,), (1,)), ((), ())),
        preferred_element_type=jnp.float32,
    )
    exponent = jnp.exp(logits)
    probs = exponent / jnp.sum(exponent, axis=0, keepdims=True)
    expert = lax.broadcasted_iota(jnp.int32, probs.shape, 0)
    hit = ids[0:1, :] == expert
    for k in range(1, ids.shape[0]):
        hit = hit | (ids[k : k + 1, :] == expert)
    chosen = jnp.where(hit, 1.0, 0.0).astype(jnp.float32)
    gates = jnp.transpose(probs * chosen).astype(jnp.bfloat16)
    for c in range(0, width, COLS):
        channel = jnp.dot(gates, load_scale(c, COLS), preferred_element_type=jnp.float32)
        mixed[0:rows, c : c + COLS] = (nrm[0:rows, c : c + COLS] * channel).astype(jnp.bfloat16)
    return (
        jnp.sum(probs, axis=1, keepdims=True),
        jnp.sum(chosen, axis=1, keepdims=True),
    )


def mix_block(rows, cur, mixed, w, n, choice=None):
    weight = w[:, n : n + WIDE]
    if choice is not None:
        weight = jnp.where(choice[0], weight, choice[1][:, n : n + WIDE])
    update = jnp.dot(mixed[0:rows, :], weight, preferred_element_type=jnp.float32)
    cur[0:rows, n : n + WIDE] = (cur[0:rows, n : n + WIDE].astype(jnp.float32) + update).astype(
        jnp.bfloat16
    )


def add_stats(stats, lane, sums, counts):
    at = lax.broadcasted_iota(jnp.int32, stats.shape, 1)
    stats[...] += jnp.where(at == lane, sums, 0.0) + jnp.where(at == lane + 1, counts, 0.0)


def relay_layer(r, cur, ids, sems=None):
    rows = cur.shape[0]
    sums, counts = front(
        rows,
        lambda c, n: cur[0:rows, c : c + n],
        lambda c, n: r["gain"][:, c : c + n],
        lambda: r["router"][...],
        lambda c, n: r["scale"][:, c : c + n],
        ids,
        r["nrm"],
        r["nbf"],
        r["mixed"],
    )
    for i, n in enumerate(range(0, cur.shape[1], WIDE)):
        if sems is not None:
            weight_copy(r, sems, i, n).wait()
        mix_block(rows, cur, r["mixed"], r["w"], n)
    return sums, counts


SMALL = ("gain", "ids", "router", "scale")


def weight_copy(r, sems, i, n):
    return pltpu.make_async_copy(
        r["w_hbm"].at[:, pl.ds(n, WIDE)], r["w"].at[:, pl.ds(n, WIDE)], sems.at[i]
    )


def small_copies(r):
    return [
        pltpu.make_async_copy(r[n + "_hbm"], r[n], r["ssem"].at[i]) for i, n in enumerate(SMALL)
    ]


def load_own(r):
    for copy in small_copies(r):
        copy.start()
    for i, n in enumerate(range(0, r["w"].shape[1], WIDE)):
        weight_copy(r, r["wsem"], i, n).start()
    for copy in small_copies(r):
        copy.wait()


def wait_weight(r):
    for i, n in enumerate(range(0, r["w"].shape[1], WIDE)):
        weight_copy(r, r["wsem"], i, n).wait()


def hidden_copies(r, t, to):
    return [
        pltpu.make_async_copy(
            r["hidden"].at[2 * t + b], to.at[pl.ds(64 * b, 64)], r["xsem"].at[b]
        )
        for b in range(2)
    ]


def step_kernel(t, names_in, names_out, names_scratch, *refs):
    ins = dict(zip(names_in, refs))
    outs = dict(zip(names_out, refs[len(names_in) :]))
    r = ins | outs | dict(zip(names_scratch, refs[len(names_in) + len(names_out) :]))
    chip, core = lax.axis_index("x"), lax.axis_index("c")
    if "stats_in" in r:
        r["stats"][...] = r["stats_in"][...]
    else:
        r["stats"][...] = jnp.zeros_like(r["stats"])

    def pair_ids(chunk):
        return jnp.concatenate([r["ids"][2 * chunk], r["ids"][2 * chunk + 1]], axis=1)

    if t == 0:

        @pl.when((chip == 0) & (core == 0))
        def _():
            for copy in hidden_copies(r, 0, r["sendR"]):
                copy.start()
            load_own(r)
            for copy in hidden_copies(r, 0, r["sendR"]):
                copy.wait()
            sums, counts = relay_layer(r, r["sendR"], pair_ids(0), r["wsem"])
            add_stats(r["stats"], 0, sums, counts)

        @pl.when((chip == 0) & (core == 1))
        def _():
            load_own(r)
            wait_weight(r)

    if t == 1:

        @pl.when(chip > 0)
        def _():
            load_own(r)
            r["small"][0:60, :] = r["router"][...]
            r["small"][64:124, :] = r["scale"][...]
            r["small"][128:129, :] = r["gain"][...]
            wait_weight(r)

    if 1 <= t < CHUNKS + 2:
        cur = r["cur"] if "cur" in r else r["sendR"]
        first, second = (chip == 0) & (core == 0), (chip == 0) & (core == 1)
        chunk = t - 2 * core
        if t < CHUNKS:

            @pl.when(first)
            def _():
                for copy in hidden_copies(r, t, cur):
                    copy.start()
                for copy in hidden_copies(r, t, cur):
                    copy.wait()

        if t >= 2:

            @pl.when(second)
            def _():
                cur[...] = r["recvR"][...]

        @pl.when(first if t < 2 else (second if t >= CHUNKS else chip == 0))
        def _():
            sums, counts = relay_layer(r, cur, pair_ids(chunk))
            add_stats(r["stats"], 2 * core, sums, counts)

        if 2 <= t < CHUNKS:

            @pl.when(first)
            def _():
                r["sendR"][...] = cur[...]

        if t >= 2:

            @pl.when(second)
            def _():
                r["sendA"][...] = cur[0:64, :]
                r["sendB"][...] = cur[64:128, :]

    if t >= 4:
        chunk = t - 2 - 2 * chip
        active = (chip >= 1) & (chunk >= 0) & (chunk < CHUNKS)

        @pl.when(active)
        def _():
            cur = r["sendB"]
            if "recvA" in r:
                from_a = (chip == 1) & (core == 0)

                @pl.when(from_a)
                def _():
                    cur[...] = r["recvA"][...]

                @pl.when(jnp.logical_not(from_a))
                def _():
                    cur[...] = r["recvB"][...]
            else:
                cur[...] = r["recvB"][...]
            batch = 2 * chunk + core

            def one(layer, carry):
                own = layer == core
                small, other = r["small"], r["small_other"]

                def pick(rows, c, n):
                    return jnp.where(own, small[rows, c : c + n], other[rows, c : c + n])

                sums, counts = front(
                    64,
                    lambda c, n: cur[:, c : c + n],
                    lambda c, n: pick(slice(128, 129), c, n),
                    lambda: pick(slice(0, 60), 0, cur.shape[1]),
                    lambda c, n: pick(slice(64, 124), c, n),
                    jnp.where(own, r["ids"][batch], r["ids_other"][batch]),
                    r["nrm"],
                    r["nbf"],
                    r["mixed"],
                )
                for n in range(0, cur.shape[1], WIDE):
                    mix_block(64, cur, r["mixed"], r["w"], n, (own, r["w_other"]))

                add_stats(r["stats"], 2 * layer, sums, counts)
                return carry

            lax.fori_loop(0, 2, one, 0)


    if t == STEPS - 1:
        table = jnp.transpose(
            jnp.concatenate([r["stats"][...], jnp.zeros((128 - 60, 128), jnp.float32)], axis=0)
        )
        for layer in range(2):
            row = table[2 * layer : 2 * layer + 1, :]
            counts = table[2 * layer + 1 : 2 * layer + 2, :]
            at = lax.broadcasted_iota(jnp.int32, row.shape, 1)
            row = jnp.where(at < 60, row, jnp.where(at >= 64, pltpu.roll(counts, 64, 1), 0.0))
            r["table"][32 * layer : 32 * layer + 32, :] = jnp.broadcast_to(row, (32, 128))


def final_kernel(token_total, *refs):
    arrived, parts, last, out, balance, sem = refs[0], refs[1:4], refs[4], *refs[5:8]
    chip = lax.axis_index("x")
    for k, part in enumerate((*parts, last)):

        @pl.when(chip == k)
        def _():
            pltpu.make_async_copy(part, out, sem).start()

    total = jnp.sum(arrived[...], axis=0, keepdims=True)
    counts = pltpu.roll(total, 64, 1)
    at = lax.broadcasted_iota(jnp.int32, total.shape, 1)
    terms = jnp.where(at < 60, (counts / (token_total * 4.0)) * (total / token_total), 0.0)
    balance[0] = 60.0 * jnp.sum(terms)
    pltpu.make_async_copy(last, out, sem).wait()


def call(kernel, ins, outs, scratch, flops, aliases=()):
    names_in, names_out = tuple(ins), tuple(outs)
    space = {n: pltpu.HBM if n.endswith("_hbm") or n == "hidden" else pltpu.VMEM for n in ins}
    args = [pltpu.with_memory_space_constraint(ins[n], space[n]) for n in names_in]
    place = {"out": pltpu.HBM, "balance": pltpu.SMEM}
    out_space = {n: place.get(n, pltpu.VMEM) for n in outs}
    got = pl.pallas_call(
        kernel,
        out_shape=[out_space[n](*outs[n]) for n in names_out],
        in_specs=[pl.BlockSpec(memory_space=space[n]) for n in names_in],
        out_specs=[pl.BlockSpec(memory_space=out_space[n]) for n in names_out],
        scratch_shapes=list(scratch.values()),
        input_output_aliases={names_in.index(a): names_out.index(b) for a, b in aliases},
        compiler_params=pltpu.CompilerParams(vmem_limit_bytes=VMEM_LIMIT),
        cost_estimate=pl.CostEstimate(
            flops=flops, bytes_accessed=8 * 1024 * 1024, transcendentals=0
        ),
    )(*args)
    return dict(zip(names_out, got))


def run_step(t, ins, outs, aliases=()):
    rows = 128 if t < CHUNKS + 2 else 64
    scratch = {
        "nrm": pltpu.VMEM((rows, 2048), jnp.float32),
        "nbf": pltpu.VMEM((rows, 2048), jnp.bfloat16),
        "mixed": pltpu.VMEM((rows, 2048), jnp.bfloat16),
    }
    if 2 <= t < CHUNKS + 2:
        scratch["cur"] = pltpu.VMEM((128, 2048), jnp.bfloat16)
    if t < CHUNKS:
        scratch["xsem"] = pltpu.SemaphoreType.DMA((2,))
    if "stats" not in outs:
        scratch["stats"] = pltpu.VMEM((60, 128), jnp.float32)
    if t < 2:
        scratch["wsem"] = pltpu.SemaphoreType.DMA((4,))
        scratch["ssem"] = pltpu.SemaphoreType.DMA((4,))
    kernel = functools.partial(step_kernel, t, tuple(ins), tuple(outs), tuple(scratch))
    return call(kernel, ins, outs, scratch, 2 * 64 * 2048 * 2048 * 2, aliases)


def hop_pairs(t):
    pairs = []
    if 2 <= t < CHUNKS + 2:
        pairs.append((1, 3))
    for chip in (1, 2, 3):
        chunk = t - 2 - 2 * chip
        if 0 <= chunk < CHUNKS:
            goal = chip + 1 if chip < CHIPS - 1 else chunk
            if goal != chip or chip < CHIPS - 1:
                pairs += [(2 * chip + c, 2 * goal + c) for c in range(2)]
    return pairs


def per_device(hidden_in, norm_gain, router_weight, expert_scale, mix_weight, routes):
    batches, rows, width = hidden_in.shape
    experts = router_weight.shape[2]
    router = jnp.transpose(router_weight[0])
    ids = jnp.transpose(routes[0], (0, 2, 1))
    scale, w = expert_scale[0], mix_weight[0]
    swap = [(2 * x + c, 2 * x + 1 - c) for x in range(1, CHIPS) for c in range(2)]

    def hop(x, pairs):
        return lax.ppermute(x, SEC, pairs)

    half = ((rows, width), jnp.bfloat16)
    full = ((2 * rows, width), jnp.bfloat16)
    stats_shape = ((experts, 128), jnp.float32)
    own = {"w": w, "router": router, "scale": scale, "gain": norm_gain, "ids": ids}
    own_hbm = {n + "_hbm": v for n, v in own.items()}
    own_shapes = {n: (v.shape, v.dtype) for n, v in own.items()}
    got = run_step(
        0,
        {"hidden": hidden_in, **own_hbm},
        {**own_shapes, "sendR": full, "stats": stats_shape},
    )
    recv = {("R", 0): hop(got["sendR"], [(0, 1)])}
    w_other = hop(w, swap)
    ids_other = hop(ids, swap)
    got = run_step(
        1,
        {
            "stats_in": got["stats"],
            "hidden": hidden_in,
            **own_hbm,
            **{n + "_in": got[n] for n in own},
        },
        {**own_shapes, "sendR": full, "stats": stats_shape, "small": ((144, width), jnp.bfloat16)},
        [(n + "_in", n) for n in own],
    )
    recv[("R", 1)] = hop(got["sendR"], [(0, 1)])
    small, stats, own = got["small"], got["stats"], {n: got[n] for n in own}
    small_other = hop(small, swap)
    last = None
    for t in range(2, STEPS):
        ins = {"stats_in": stats, "ids": own["ids"], "w": own["w"]}
        outs = {"stats": stats_shape, "sendB": half}
        if t < CHUNKS + 2:
            ins |= own
            ins["recvR"] = recv[("R", t - 2)]
            outs["sendA"] = half
        if t < CHUNKS:
            ins["hidden"] = hidden_in
            outs["sendR"] = full
        if t >= 4:
            ins |= {"small": small, "small_other": small_other}
            ins |= {"w_other": w_other, "ids_other": ids_other}
            ins["recvB"] = recv[("B", t - 2)]
            if ("A", t - 2) in recv:
                ins["recvA"] = recv[("A", t - 2)]
        if t == STEPS - 1:
            outs = {"sendB": half, "table": ((2 * 32, 128), jnp.float32)}
        got = run_step(t, ins, outs)
        stats, last = got.get("stats"), got["sendB"]
        if t < STEPS - 1:
            recv[("B", t)] = hop(got["sendB"], hop_pairs(t))
        if 2 <= t < CHUNKS + 2:
            recv[("A", t)] = hop(got["sendA"], [(1, 2)])
        if t < CHUNKS:
            recv[("R", t)] = hop(got["sendR"], [(0, 1)])
    arrived = lax.all_to_all(got["table"], ("c", "z", "y"), 0, 0, tiled=True)
    token_total = float(batches * rows * lax.axis_size("z") * lax.axis_size("y"))
    got = call(
        functools.partial(final_kernel, token_total),
        {
            "arrived": arrived,
            **{f"part{k}": recv[("B", k + 8)] for k in range(CHUNKS - 1)},
            "last": last,
        },
        {"out": half, "balance": ((1,), jnp.float32)},
        {"sem": pltpu.SemaphoreType.DMA},
        1000,
    )
    return got["out"][None], got["balance"]


def solution(mesh):
    torus = Mesh(mesh.devices.reshape(CHIPS, 2, 8, 4), ("x", "c", "z", "y"))
    dp = ("z", "y")

    return jax.shard_map(
        per_device,
        mesh=torus,
        in_specs=(
            P(None, dp, None),
            P(SEC, None),
            P(SEC, None, None),
            P(SEC, None, None),
            P(SEC, None, None),
            P(SEC, None, dp, None),
        ),
        out_specs=(P(SEC, dp, None), P(SEC)),
        check_vma=False,
    )
```

profile of v0, /device:TPU:7, one launch (start us, length us, event | category | flops | bytes accessed | tf_op | source)
XLA Modules:
  0.0 96.5 jit_solution(15733050839951352919)
XLA Ops:
  0.6 2.6 %collective-permute-start.4 = (bf16[2048,2048]{1,0:T(8,128)(2,1)}, bf16[2048,2048]{1,0:T(8,128)(2,1)S(1)}, u32[]{:S(2)}, u32[]{:S(2)}) collective-permute-start(bf16[2048,2048]{1,0:T(8,128)(2,1)} %bitcast.15), channel_id=1, source_target_pairs={{64,96},{96,64},{128,160},{160,128},{192,224},{224,192},{65,97},{9... | collective-permute-start | bytes 25165832 | tf_op jit(solution)/shard_map/ppermute | solution.py:347
  3.2 0.1 shard_map.77
  3.4 0.7 collective-permute-start
  4.1 3.8 %shard_map.78 = (bf16[2048,2048]{1,0:T(8,128)(2,1)S(1)}, bf16[60,2048]{1,0:T(8,128)(2,1)S(1)}, bf16[60,2048]{1,0:T(8,128)(2,1)S(1)}, bf16[1,2048]{1,0:T(2,128)(2...) custom-call(f32[60,128]{1,0:T(8,128)S(1)} %get-tuple-element.45.refs, ...), custom_call_target="tpu_custom_call", output_to_operand_aliasing={{0}: (7, {}), {1}: (8, {}), {2}: (9, {}), {3}: (10, {}), {4... | custom-call | flops 1073741824 | bytes 8388608 | tf_op jit(solution)/shard_map/pallas_call | solution.py:290
  7.9 0.0 copy-start
  7.9 0.7 collective-permute-start.1
  8.6 1.9 %collective-permute-start.3 = (bf16[144,2048]{1,0:T(8,128)(2,1)S(1)}, bf16[144,2048]{1,0:T(8,128)(2,1)S(1)}, u32[]{:S(2)}, u32[]{:S(2)}) collective-permute-start(bf16[144,2048]{1,0:T(8,128)(2,1)S(1)} %get-tuple-element.62.refs_7_.refs_3_), channel_id=1, source_target_pairs={{64,96},{96,64},{128,160},{160,128},{192,224},{224,192},{65,97},{9... | collective-permute-start | bytes 1769480 | tf_op jit(solution)/shard_map/ppermute | solution.py:347
  10.5 0.0 collective-permute-done.refs_6_
  10.5 0.1 shard_map.79
  10.6 0.7 collective-permute-start.2
  11.3 0.0 copy-done
  11.3 2.4 %collective-permute-start.5 = (s32[8,4,64]{2,1,0:T(4,128)S(1)}, s32[8,4,64]{2,1,0:T(4,128)S(1)}, u32[]{:S(2)}, u32[]{:S(2)}) collective-permute-start(s32[8,4,64]{2,1,0:T(4,128)S(1)} %bitcast.24), channel_id=1, source_target_pairs={{64,96},{96,64},{128,160},{160,128},{192,224},{224,192},{65,97},{9... | collective-permute-start | bytes 24584 | tf_op jit(solution)/shard_map/ppermute | solution.py:347
  13.7 0.0 collective-permute-done.1.refs_6_
  13.7 0.7 collective-permute-start.6
  14.4 0.1 shard_map.80
  14.5 2.6 %collective-permute-done.5.refs_10_.refs_6_ = s32[8,4,64]{2,1,0:T(4,128)S(1)} collective-permute-done((s32[8,4,64]{2,1,0:T(4,128)S(1)}, s32[8,4,64]{2,1,0:T(4,128)S(1)}, u32[]{:S(2)}, u32[]{:S(2)}) %collective-permute-start.5) | collective-permute-done | bytes 8224 | tf_op jit(solution)/shard_map/ppermute | solution.py:347
  17.1 0.7 collective-permute-start.7
  17.7 0.0 collective-permute-done.3.refs_8_.refs_4_
  17.7 0.7 collective-permute-start.8
  18.4 0.0 collective-permute-done.6.refs_11_
  18.5 0.7 collective-permute-start.10
  19.1 0.0 collective-permute-done.7.refs_12_
  19.2 0.7 collective-permute-start.9
  19.8 0.0 collective-permute-done.2.refs_6_
  19.9 0.0 collective-permute-done.4.refs_9_.refs_5_
  19.9 0.2 shard_map.81
  20.1 0.7 collective-permute-start.11
  20.8 0.7 collective-permute-start.12
  21.4 0.0 collective-permute-done.10.refs_12_
  21.5 0.0 collective-permute-done.9.refs_11_
  21.5 0.0 collective-permute-done.8.refs_6_
  21.5 0.7 collective-permute-start.13
  22.2 0.7 collective-permute-start.14
  22.9 0.0 collective-permute-done.11.refs_7_
  22.9 0.0 collective-permute-done.12.refs_8_
  22.9 1.3 %collective-permute-start.15 = (bf16[64,2048]{1,0:T(8,128)(2,1)S(1)}, bf16[64,2048]{1,0:T(8,128)(2,1)S(1)}, u32[]{:S(2)}, u32[]{:S(2)}) collective-permute-start(bf16[64,2048]{1,0:T(8,128)(2,1)S(1)} %get-tuple-element.76), channel_id=1, source_target_pairs={{64,128},{96,160},{128,192},{160,224},{65,129},{97,161},{129,193},... | collective-permute-start | bytes 786440 | tf_op jit(solution)/shard_map/ppermute | solution.py:347
  24.2 0.0 collective-permute-done.13.refs_7_
  24.3 0.0 collective-permute-done.14.refs_8_
  24.3 1.3 %collective-permute-start.16 = (bf16[64,2048]{1,0:T(8,128)(2,1)S(1)}, bf16[64,2048]{1,0:T(8,128)(2,1)S(1)}, u32[]{:S(2)}, u32[]{:S(2)}) collective-permute-start(bf16[64,2048]{1,0:T(8,128)(2,1)S(1)} %get-tuple-element.78), channel_id=1, source_target_pairs={{64,128},{96,160},{128,192},{160,224},{65,129},{97,161},{129,193},... | collective-permute-start | bytes 786440 | tf_op jit(solution)/shard_map/ppermute | solution.py:347
  25.6 21.3 %collective-permute-done.15.refs_7_ = bf16[64,2048]{1,0:T(8,128)(2,1)S(1)} collective-permute-done((bf16[64,2048]{1,0:T(8,128)(2,1)S(1)}, bf16[64,2048]{1,0:T(8,128)(2,1)S(1)}, u32[]{:S(2)}, u32[]{:S(2)}) %collective-permute-start.15) | collective-permute-done | bytes 262176 | tf_op jit(solution)/shard_map/ppermute | solution.py:347
  46.9 4.4 %shard_map.85 = (f32[60,128]{1,0:T(8,128)S(1)}, bf16[64,2048]{1,0:T(8,128)(2,1)S(1)}) custom-call(f32[60,128]{1,0:T(8,128)S(1)} %get-tuple-element.75.refs_0_, s32[8,4,64]{2,1,0:T(4,128)S(1)} %get-tuple-element.52.refs_1_, bf16[2048,2048]{1,0:T(8,128)(2,1)S(1)} %get-tuple-element.53.refs_2_, bf16[144,2048]{1,0:T(8,128)(2,1)S(1)} %get-tuple-element.62.refs_7_.refs_3_, ...), custom_call_target="tpu_custom_call" | custom-call | flops 1073741824 | bytes 8388608 | tf_op jit(solution)/shard_map/pallas_call | solution.py:290
  51.4 1.9 %collective-permute-start.17 = (bf16[64,2048]{1,0:T(8,128)(2,1)S(1)}, bf16[64,2048]{1,0:T(8,128)(2,1)S(1)}, u32[]{:S(2)}, u32[]{:S(2)}) collective-permute-start(bf16[64,2048]{1,0:T(8,128)(2,1)S(1)} %get-tuple-element.80), channel_id=1, source_target_pairs={{128,192},{160,224},{192,0},{224,32},{129,193},{161,225},{193,1},{... | collective-permute-start | bytes 786440 | tf_op jit(solution)/shard_map/ppermute | solution.py:347
  53.3 0.8 collective-permute-done.16.refs_7_
  54.1 4.4 %shard_map.86 = (f32[60,128]{1,0:T(8,128)S(1)}, bf16[64,2048]{1,0:T(8,128)(2,1)S(1)}) custom-call(f32[60,128]{1,0:T(8,128)S(1)} %get-tuple-element.77.refs_0_, s32[8,4,64]{2,1,0:T(4,128)S(1)} %get-tuple-element.52.refs_1_, bf16[2048,2048]{1,0:T(8,128)(2,1)S(1)} %get-tuple-element.53.refs_2_, bf16[144,2048]{1,0:T(8,128)(2,1)S(1)} %get-tuple-element.62.refs_7_.refs_3_, ...), custom_call_target="tpu_custom_call" | custom-call | flops 1073741824 | bytes 8388608 | tf_op jit(solution)/shard_map/pallas_call | solution.py:290
  58.6 1.9 %collective-permute-start.18 = (bf16[64,2048]{1,0:T(8,128)(2,1)S(1)}, bf16[64,2048]{1,0:T(8,128)(2,1)S(1)}, u32[]{:S(2)}, u32[]{:S(2)}) collective-permute-start(bf16[64,2048]{1,0:T(8,128)(2,1)S(1)} %get-tuple-element.82), channel_id=1, source_target_pairs={{128,192},{160,224},{192,64},{224,96},{129,193},{161,225},{193,65}... | collective-permute-start | bytes 786440 | tf_op jit(solution)/shard_map/ppermute | solution.py:347
  60.5 0.0 collective-permute-done.17.refs_7_.refs_1_
  60.5 4.5 %shard_map.87 = (f32[60,128]{1,0:T(8,128)S(1)}, bf16[64,2048]{1,0:T(8,128)(2,1)S(1)}) custom-call(f32[60,128]{1,0:T(8,128)S(1)} %get-tuple-element.79.refs_0_, s32[8,4,64]{2,1,0:T(4,128)S(1)} %get-tuple-element.52.refs_1_, bf16[2048,2048]{1,0:T(8,128)(2,1)S(1)} %get-tuple-element.53.refs_2_, bf16[144,2048]{1,0:T(8,128)(2,1)S(1)} %get-tuple-element.62.refs_7_.refs_3_, ...), custom_call_target="tpu_custom_call" | custom-call | flops 1073741824 | bytes 8388608 | tf_op jit(solution)/shard_map/pallas_call | solution.py:290
  65.0 1.5 %collective-permute-start.19 = (bf16[64,2048]{1,0:T(8,128)(2,1)S(1)}, bf16[64,2048]{1,0:T(8,128)(2,1)S(1)}, u32[]{:S(2)}, u32[]{:S(2)}) collective-permute-start(bf16[64,2048]{1,0:T(8,128)(2,1)S(1)} %get-tuple-element.84), channel_id=1, source_target_pairs={{192,128},{224,160},{193,129},{225,161},{194,130},{226,162},{195,1... | collective-permute-start | bytes 786440 | tf_op jit(solution)/shard_map/ppermute | solution.py:347
  66.5 0.1 collective-permute-done.18.refs_7_.refs_2_
  66.6 4.6 %shard_map.88 = (bf16[64,2048]{1,0:T(8,128)(2,1)S(1)}, f32[64,128]{1,0:T(8,128)S(1)}) custom-call(f32[60,128]{1,0:T(8,128)S(1)} %get-tuple-element.81.refs_0_, s32[8,4,64]{2,1,0:T(4,128)S(1)} %get-tuple-element.52.refs_1_, bf16[2048,2048]{1,0:T(8,128)(2,1)S(1)} %get-tuple-element.53.refs_2_, bf16[144,2048]{1,0:T(8,128)(2,1)S(1)} %get-tuple-element.62.refs_7_.refs_3_, ...), custom_call_target="tpu_custom_call" | custom-call | flops 1073741824 | bytes 8388608 | tf_op jit(solution)/shard_map/pallas_call | solution.py:290
  71.2 23.8 %all_to_all.11 = f32[64,1,128]{2,1,0:T(1,128)S(1)} all-to-all(f32[64,1,128]{2,1,0:T(1,128)S(1)} %bitcast.14), channel_id=1, replica_groups=mesh['x'=4,'c'=2,'z'=8,'y'=4] {'c','z','y'}, dimensions={0} | all-to-all | bytes 65536 | tf_op jit(solution)/shard_map/all_to_all | solution.py:404
  95.1 0.0 collective-permute-done.19.refs_3_
  95.1 0.7 shard_map.89
  (3 shorter events, 0.1 us)
Async XLA Ops:
  0.6 19.2 %collective-permute-start.4 = (bf16[2048,2048]{1,0:T(8,128)(2,1)}, bf16[2048,2048]{1,0:T(8,128)(2,1)S(1)}, u32[]{:S(2)}, u32[]{:S(2)}) collective-permute-start(bf16[2048,2048]{1,0:T(8,128)(2,1)} %bitcast.15), channel_id=1, source_target_pairs={{64,96},{96,64},{128,160},{160,128},{192,224},{224,192},{65,97},{9... | collective-permute-start | bytes 25165832 | tf_op jit(solution)/shard_map/ppermute | solution.py:347
  3.4 7.2 %collective-permute-start = (bf16[128,2048]{1,0:T(8,128)(2,1)S(1)}, bf16[128,2048]{1,0:T(8,128)(2,1)S(1)}, u32[]{:S(2)}, u32[]{:S(2)}) collective-permute-start(bf16[128,2048]{1,0:T(8,128)(2,1)S(1)} %get-tuple-element.57), channel_id=1, source_target_pairs={{0,32},{1,33},{2,34},{3,35},{4,36},{5,37},{6,38},{7,39},{8,40},{9,... | collective-permute-start | bytes 1572872 | tf_op jit(solution)/shard_map/ppermute | solution.py:347
  7.9 3.4 %copy-start = (s32[1,8,64,4]{2,3,1,0:T(4,128)S(1)}, s32[1,8,64,4]{2,3,1,0:T(4,128)}, u32[]{:S(2)}) copy-start(s32[1,8,64,4]{2,3,1,0:T(4,128)} %param.11) | copy-start | bytes 24580
  7.9 5.8 %collective-permute-start.1 = (bf16[128,2048]{1,0:T(8,128)(2,1)S(1)}, bf16[128,2048]{1,0:T(8,128)(2,1)S(1)}, u32[]{:S(2)}, u32[]{:S(2)}) collective-permute-start(bf16[128,2048]{1,0:T(8,128)(2,1)S(1)} %get-tuple-element.59), channel_id=1, source_target_pairs={{0,32},{1,33},{2,34},{3,35},{4,36},{5,37},{6,38},{7,39},{8,40},{9,... | collective-permute-start | bytes 1572872 | tf_op jit(solution)/shard_map/ppermute | solution.py:347
  8.6 9.2 %collective-permute-start.3 = (bf16[144,2048]{1,0:T(8,128)(2,1)S(1)}, bf16[144,2048]{1,0:T(8,128)(2,1)S(1)}, u32[]{:S(2)}, u32[]{:S(2)}) collective-permute-start(bf16[144,2048]{1,0:T(8,128)(2,1)S(1)} %get-tuple-element.62.refs_7_.refs_3_), channel_id=1, source_target_pairs={{64,96},{96,64},{128,160},{160,128},{192,224},{224,192},{65,97},{9... | collective-permute-start | bytes 1769480 | tf_op jit(solution)/shard_map/ppermute | solution.py:347
  10.6 9.3 %collective-permute-start.2 = (bf16[128,2048]{1,0:T(8,128)(2,1)S(1)}, bf16[128,2048]{1,0:T(8,128)(2,1)S(1)}, u32[]{:S(2)}, u32[]{:S(2)}) collective-permute-start(bf16[128,2048]{1,0:T(8,128)(2,1)S(1)} %get-tuple-element.61), channel_id=1, source_target_pairs={{0,32},{1,33},{2,34},{3,35},{4,36},{5,37},{6,38},{7,39},{8,40},{9,... | collective-permute-start | bytes 1572872 | tf_op jit(solution)/shard_map/ppermute | solution.py:347
  11.3 5.8 %collective-permute-start.5 = (s32[8,4,64]{2,1,0:T(4,128)S(1)}, s32[8,4,64]{2,1,0:T(4,128)S(1)}, u32[]{:S(2)}, u32[]{:S(2)}) collective-permute-start(s32[8,4,64]{2,1,0:T(4,128)S(1)} %bitcast.24), channel_id=1, source_target_pairs={{64,96},{96,64},{128,160},{160,128},{192,224},{224,192},{65,97},{9... | collective-permute-start | bytes 24584 | tf_op jit(solution)/shard_map/ppermute | solution.py:347
  13.7 4.7 %collective-permute-start.6 = (bf16[64,2048]{1,0:T(8,128)(2,1)S(1)}, bf16[64,2048]{1,0:T(8,128)(2,1)S(1)}, u32[]{:S(2)}, u32[]{:S(2)}) collective-permute-start(bf16[64,2048]{1,0:T(8,128)(2,1)S(1)} %get-tuple-element.63), channel_id=1, source_target_pairs={{32,96},{33,97},{34,98},{35,99},{36,100},{37,101},{38,102},{39,103... | collective-permute-start | bytes 786440 | tf_op jit(solution)/shard_map/ppermute | solution.py:347
  17.1 2.1 %collective-permute-start.7 = (bf16[64,2048]{1,0:T(8,128)(2,1)S(1)}, bf16[64,2048]{1,0:T(8,128)(2,1)S(1)}, u32[]{:S(2)}, u32[]{:S(2)}) collective-permute-start(bf16[64,2048]{1,0:T(8,128)(2,1)S(1)} %get-tuple-element.64), channel_id=1, source_target_pairs={{32,64},{33,65},{34,66},{35,67},{36,68},{37,69},{38,70},{39,71},{4... | collective-permute-start | bytes 786440 | tf_op jit(solution)/shard_map/ppermute | solution.py:347
  17.7 3.7 %collective-permute-start.8 = (bf16[128,2048]{1,0:T(8,128)(2,1)S(1)}, bf16[128,2048]{1,0:T(8,128)(2,1)S(1)}, u32[]{:S(2)}, u32[]{:S(2)}) collective-permute-start(bf16[128,2048]{1,0:T(8,128)(2,1)S(1)} %get-tuple-element.66), channel_id=1, source_target_pairs={{0,32},{1,33},{2,34},{3,35},{4,36},{5,37},{6,38},{7,39},{8,40},{9,... | collective-permute-start | bytes 1572872 | tf_op jit(solution)/shard_map/ppermute | solution.py:347
  18.5 3.0 %collective-permute-start.10 = (bf16[64,2048]{1,0:T(8,128)(2,1)S(1)}, bf16[64,2048]{1,0:T(8,128)(2,1)S(1)}, u32[]{:S(2)}, u32[]{:S(2)}) collective-permute-start(bf16[64,2048]{1,0:T(8,128)(2,1)S(1)} %get-tuple-element.68), channel_id=1, source_target_pairs={{32,64},{33,65},{34,66},{35,67},{36,68},{37,69},{38,70},{39,71},{4... | collective-permute-start | bytes 786440 | tf_op jit(solution)/shard_map/ppermute | solution.py:347
  19.2 2.3 %collective-permute-start.9 = (bf16[64,2048]{1,0:T(8,128)(2,1)S(1)}, bf16[64,2048]{1,0:T(8,128)(2,1)S(1)}, u32[]{:S(2)}, u32[]{:S(2)}) collective-permute-start(bf16[64,2048]{1,0:T(8,128)(2,1)S(1)} %get-tuple-element.67), channel_id=1, source_target_pairs={{32,96},{33,97},{34,98},{35,99},{36,100},{37,101},{38,102},{39,103... | collective-permute-start | bytes 786440 | tf_op jit(solution)/shard_map/ppermute | solution.py:347
  20.1 2.8 %collective-permute-start.11 = (bf16[64,2048]{1,0:T(8,128)(2,1)S(1)}, bf16[64,2048]{1,0:T(8,128)(2,1)S(1)}, u32[]{:S(2)}, u32[]{:S(2)}) collective-permute-start(bf16[64,2048]{1,0:T(8,128)(2,1)S(1)} %get-tuple-element.70), channel_id=1, source_target_pairs={{32,96},{64,128},{96,160},{33,97},{65,129},{97,161},{34,98},{66,13... | collective-permute-start | bytes 786440 | tf_op jit(solution)/shard_map/ppermute | solution.py:347
  20.8 2.1 %collective-permute-start.12 = (bf16[64,2048]{1,0:T(8,128)(2,1)S(1)}, bf16[64,2048]{1,0:T(8,128)(2,1)S(1)}, u32[]{:S(2)}, u32[]{:S(2)}) collective-permute-start(bf16[64,2048]{1,0:T(8,128)(2,1)S(1)} %get-tuple-element.71), channel_id=1, source_target_pairs={{32,64},{33,65},{34,66},{35,67},{36,68},{37,69},{38,70},{39,71},{4... | collective-permute-start | bytes 786440 | tf_op jit(solution)/shard_map/ppermute | solution.py:347
  21.5 2.7 %collective-permute-start.13 = (bf16[64,2048]{1,0:T(8,128)(2,1)S(1)}, bf16[64,2048]{1,0:T(8,128)(2,1)S(1)}, u32[]{:S(2)}, u32[]{:S(2)}) collective-permute-start(bf16[64,2048]{1,0:T(8,128)(2,1)S(1)} %get-tuple-element.73), channel_id=1, source_target_pairs={{32,96},{64,128},{96,160},{33,97},{65,129},{97,161},{34,98},{66,13... | collective-permute-start | bytes 786440 | tf_op jit(solution)/shard_map/ppermute | solution.py:347
  22.2 2.0 %collective-permute-start.14 = (bf16[64,2048]{1,0:T(8,128)(2,1)S(1)}, bf16[64,2048]{1,0:T(8,128)(2,1)S(1)}, u32[]{:S(2)}, u32[]{:S(2)}) collective-permute-start(bf16[64,2048]{1,0:T(8,128)(2,1)S(1)} %get-tuple-element.74), channel_id=1, source_target_pairs={{32,64},{33,65},{34,66},{35,67},{36,68},{37,69},{38,70},{39,71},{4... | collective-permute-start | bytes 786440 | tf_op jit(solution)/shard_map/ppermute | solution.py:347
  22.9 24.0 %collective-permute-start.15 = (bf16[64,2048]{1,0:T(8,128)(2,1)S(1)}, bf16[64,2048]{1,0:T(8,128)(2,1)S(1)}, u32[]{:S(2)}, u32[]{:S(2)}) collective-permute-start(bf16[64,2048]{1,0:T(8,128)(2,1)S(1)} %get-tuple-element.76), channel_id=1, source_target_pairs={{64,128},{96,160},{128,192},{160,224},{65,129},{97,161},{129,193},... | collective-permute-start | bytes 786440 | tf_op jit(solution)/shard_map/ppermute | solution.py:347
  24.3 29.8 %collective-permute-start.16 = (bf16[64,2048]{1,0:T(8,128)(2,1)S(1)}, bf16[64,2048]{1,0:T(8,128)(2,1)S(1)}, u32[]{:S(2)}, u32[]{:S(2)}) collective-permute-start(bf16[64,2048]{1,0:T(8,128)(2,1)S(1)} %get-tuple-element.78), channel_id=1, source_target_pairs={{64,128},{96,160},{128,192},{160,224},{65,129},{97,161},{129,193},... | collective-permute-start | bytes 786440 | tf_op jit(solution)/shard_map/ppermute | solution.py:347
  51.4 9.1 %collective-permute-start.17 = (bf16[64,2048]{1,0:T(8,128)(2,1)S(1)}, bf16[64,2048]{1,0:T(8,128)(2,1)S(1)}, u32[]{:S(2)}, u32[]{:S(2)}) collective-permute-start(bf16[64,2048]{1,0:T(8,128)(2,1)S(1)} %get-tuple-element.80), channel_id=1, source_target_pairs={{128,192},{160,224},{192,0},{224,32},{129,193},{161,225},{193,1},{... | collective-permute-start | bytes 786440 | tf_op jit(solution)/shard_map/ppermute | solution.py:347
  58.6 8.1 %collective-permute-start.18 = (bf16[64,2048]{1,0:T(8,128)(2,1)S(1)}, bf16[64,2048]{1,0:T(8,128)(2,1)S(1)}, u32[]{:S(2)}, u32[]{:S(2)}) collective-permute-start(bf16[64,2048]{1,0:T(8,128)(2,1)S(1)} %get-tuple-element.82), channel_id=1, source_target_pairs={{128,192},{160,224},{192,64},{224,96},{129,193},{161,225},{193,65}... | collective-permute-start | bytes 786440 | tf_op jit(solution)/shard_map/ppermute | solution.py:347
  65.0 30.1 %collective-permute-start.19 = (bf16[64,2048]{1,0:T(8,128)(2,1)S(1)}, bf16[64,2048]{1,0:T(8,128)(2,1)S(1)}, u32[]{:S(2)}, u32[]{:S(2)}) collective-permute-start(bf16[64,2048]{1,0:T(8,128)(2,1)S(1)} %get-tuple-element.84), channel_id=1, source_target_pairs={{192,128},{224,160},{193,129},{225,161},{194,130},{226,162},{195,1... | collective-permute-start | bytes 786440 | tf_op jit(solution)/shard_map/ppermute | solution.py:347
where the time goes:
time: 97 us; the launch traced here: 96.5 us
  waiting for transfers between devices  24.9 us (26%)
  blocking collectives  23.8 us (25%)
  starting transfers between devices  23 us (24%)
  Pallas kernels  23 us (24%)
  between operations  1.71 us (2%)
    ppermute x20, waiting for transfers between devices, hop(): return lax.ppermute(x, SEC, pairs)  24.9 us
    all_to_all x1, blocking collectives, per_device(): arrived = lax.all_to_all(got['table'], ('c', 'z', 'y'), 0, 0, tiled=True)  23.8 us
    ppermute x20, starting transfers between devices, hop(): return lax.ppermute(x, SEC, pairs)  23 us
    pallas_call x13, Pallas kernels, call(): pl.pallas_call(kernel, out_shape=[out_space[n](*outs[n]) for n in names_o...  23 us
  transfers between devices with their start and end apart: 20, of which 4 were waited for; matrix products, arithmetic and copies ran while one was open for 0% of the time, Pallas kernels for 23%

commit v1 on v0

v1 whole, which is shorter than its diff:
```python
import functools

import jax
import jax.numpy as jnp
from jax import lax
from jax.experimental import pallas as pl
from jax.experimental.pallas import tpu as pltpu
from jax.sharding import Mesh
from jax.sharding import PartitionSpec as P


SEC = ("x", "c")
CHIPS = 4
CHUNKS = 4
STEPS = 13
LAST_RELAY = 7
FIRST_PAIR = 5
COLS = 256
WIDE = 512
VMEM_LIMIT = 12 * 1024 * 1024


def front(rows, load_x, load_gain, load_router, load_scale, ids, nrm, nbf, mixed):
    width = nrm.shape[1]
    acc = None
    for c in range(0, width, COLS):
        xs = load_x(c, COLS).astype(jnp.float32)
        acc = xs * xs if acc is None else acc + xs * xs
    mean_square = jnp.sum(acc, axis=-1, keepdims=True) * jnp.float32(1.0 / width)
    inv = lax.rsqrt(mean_square + 1e-06)
    for c in range(0, width, COLS):
        xs = load_x(c, COLS).astype(jnp.float32)
        normed = xs * inv * load_gain(c, COLS).astype(jnp.float32)
        nrm[0:rows, c : c + COLS] = normed
        nbf[0:rows, c : c + COLS] = normed.astype(jnp.bfloat16)
    logits = lax.dot_general(
        load_router(),
        nbf[0:rows, :],
        (((1,), (1,)), ((), ())),
        preferred_element_type=jnp.float32,
    )
    exponent = jnp.exp(logits)
    probs = exponent / jnp.sum(exponent, axis=0, keepdims=True)
    expert = lax.broadcasted_iota(jnp.int32, probs.shape, 0)
    hit = ids[0:1, :] == expert
    for k in range(1, ids.shape[0]):
        hit = hit | (ids[k : k + 1, :] == expert)
    chosen = jnp.where(hit, 1.0, 0.0).astype(jnp.float32)
    gates = jnp.transpose(probs * chosen).astype(jnp.bfloat16)
    for c in range(0, width, COLS):
        channel = jnp.dot(gates, load_scale(c, COLS), preferred_element_type=jnp.float32)
        mixed[0:rows, c : c + COLS] = (nrm[0:rows, c : c + COLS] * channel).astype(jnp.bfloat16)
    return (
        jnp.sum(probs, axis=1, keepdims=True),
        jnp.sum(chosen, axis=1, keepdims=True),
    )


def mix_block(rows, cur, mixed, w, n, choice=None):
    weight = w[:, n : n + WIDE]
    if choice is not None:
        weight = jnp.where(choice[0], weight, choice[1][:, n : n + WIDE])
    update = jnp.dot(mixed[0:rows, :], weight, preferred_element_type=jnp.float32)
    cur[0:rows, n : n + WIDE] = (cur[0:rows, n : n + WIDE].astype(jnp.float32) + update).astype(
        jnp.bfloat16
    )


def add_stats(stats, lane, sums, counts):
    at = lax.broadcasted_iota(jnp.int32, stats.shape, 1)
    stats[...] += jnp.where(at == lane, sums, 0.0) + jnp.where(at == lane + 1, counts, 0.0)


def relay_layer(r, cur, ids, sems=None):
    rows = cur.shape[0]
    sums, counts = front(
        rows,
        lambda c, n: cur[0:rows, c : c + n],
        lambda c, n: r["gain"][:, c : c + n],
        lambda: r["router"][...],
        lambda c, n: r["scale"][:, c : c + n],
        ids,
        r["nrm"],
        r["nbf"],
        r["mixed"],
    )
    if rows > 64:

        def block(i, carry):
            at = pl.ds(pl.multiple_of(i * WIDE, WIDE), WIDE)
            update = jnp.dot(
                r["mixed"][0:rows, :], r["w"][:, at], preferred_element_type=jnp.float32
            )
            cur[0:rows, at] = (cur[0:rows, at].astype(jnp.float32) + update).astype(jnp.bfloat16)
            return carry

        lax.fori_loop(0, cur.shape[1] // WIDE, block, 0)
        return sums, counts
    for i, n in enumerate(range(0, cur.shape[1], WIDE)):
        if sems is not None:
            weight_copy(r, sems, i, n).wait()
        mix_block(rows, cur, r["mixed"], r["w"], n)
    return sums, counts


SMALL = ("gain", "ids", "router", "scale")


def weight_copy(r, sems, i, n):
    return pltpu.make_async_copy(
        r["w_hbm"].at[:, pl.ds(n, WIDE)], r["w"].at[:, pl.ds(n, WIDE)], sems.at[i]
    )


def weight_copies(r):
    width = r["w"].shape[1]
    return [weight_copy(r, r["wsem"], i, n) for i, n in enumerate(range(0, width, WIDE))]


def small_copies(r):
    return [
        pltpu.make_async_copy(r[n + "_hbm"], r[n], r["ssem"].at[i]) for i, n in enumerate(SMALL)
    ]


def hidden_copies(r, first, to):
    return [
        pltpu.make_async_copy(
            r["hidden"].at[first + b], to.at[pl.ds(64 * b, 64)], r["xsem"].at[b]
        )
        for b in range(to.shape[0] // 64)
    ]


def load_hidden(r, first, to):
    for copy in hidden_copies(r, first, to):
        copy.start()
    for copy in hidden_copies(r, first, to):
        copy.wait()


def pair_ids(r, chunk):
    return jnp.concatenate([r["ids"][2 * chunk], r["ids"][2 * chunk + 1]], axis=1)


def first_step(r, first, second):
    for copy in small_copies(r):
        copy.start()

    @pl.when(first)
    def _():
        load_hidden(r, 0, r["sendR"])

    for copy in small_copies(r):
        copy.wait()

    @pl.when(first | second)
    def _():
        for copy in weight_copies(r):
            copy.start()

    @pl.when(first)
    def _():
        sums, counts = relay_layer(r, r["sendR"], r["ids"][0], r["wsem"])
        add_stats(r["stats"], 0, sums, counts)

    @pl.when(second)
    def _():
        for copy in weight_copies(r):
            copy.wait()

    @pl.when(jnp.logical_not(first | second))
    def _():
        ids = jnp.concatenate([r["ids"][m] for m in range(r["ids"].shape[0])], axis=0)
        r["small"][0:60, :] = r["router"][...]
        r["small"][64:124, :] = r["scale"][...]
        r["small"][128:129, :] = r["gain"][...]
        r["small"][144:176, 0:64] = ids.astype(jnp.float32).astype(jnp.bfloat16)


def relay_step(t, r, first, second, core):
    if t == 1:

        @pl.when(first)
        def _():
            load_hidden(r, 1, r["sendR"])
            sums, counts = relay_layer(r, r["sendR"], r["ids"][1])
            add_stats(r["stats"], 0, sums, counts)

    if t in (2, 3):

        @pl.when(first)
        def _():
            load_hidden(r, 2 * (t - 1), r["sendR"])
            sums, counts = relay_layer(r, r["sendR"], pair_ids(r, t - 1))
            add_stats(r["stats"], 0, sums, counts)

        @pl.when(second)
        def _():
            cur = r["sendA"] if t == 2 else r["sendB"]
            cur[...] = r["recvR"][...]
            sums, counts = relay_layer(r, cur, r["ids"][t - 2])
            add_stats(r["stats"], 2, sums, counts)

    if 4 <= t < LAST_RELAY:
        cur = r["cur"]
        if t == 4:

            @pl.when(first)
            def _():
                load_hidden(r, 2 * (t - 1), cur)

        @pl.when(second)
        def _():
            cur[...] = r["recvR"][...]

        @pl.when((first | second) if t == 4 else second)
        def _():
            sums, counts = relay_layer(r, cur, pair_ids(r, t - 1 - 2 * core))
            add_stats(r["stats"], 2 * core, sums, counts)

        if t == 4:

            @pl.when(first)
            def _():
                r["sendR"][...] = cur[...]

        @pl.when(second)
        def _():
            r["sendA"][...] = cur[0:64, :]
            r["sendB"][...] = cur[64:128, :]


def pair_step(t, r, chip, core):
    chunk = t - 3 - 2 * chip
    cur = r["sendB"]

    @pl.when((chip >= 1) & (chunk >= 0) & (chunk < CHUNKS))
    def _():
        if "recvA" in r:
            from_a = (chip == 1) & (core == 0)

            @pl.when(from_a)
            def _():
                cur[...] = r["recvA"][...]

            @pl.when(jnp.logical_not(from_a))
            def _():
                cur[...] = r["recvB"][...]
        else:
            cur[...] = r["recvB"][...]
        batch = 2 * chunk + core
        small, other = r["small"], r["small_other"]

        def one(layer, carry):
            own = layer == core

            def pick(rows, c, n):
                return jnp.where(own, small[rows, c : c + n], other[rows, c : c + n])

            table = pick(slice(144, 176), 0, 64).astype(jnp.float32)
            ids = table[0:4]
            for m in range(1, 8):
                ids = jnp.where(batch == m, table[4 * m : 4 * m + 4], ids)
            sums, counts = front(
                64,
                lambda c, n: cur[:, c : c + n],
                lambda c, n: pick(slice(128, 129), c, n),
                lambda: pick(slice(0, 60), 0, cur.shape[1]),
                lambda c, n: pick(slice(64, 124), c, n),
                ids.astype(jnp.int32),
                r["nrm"],
                r["nbf"],
                r["mixed"],
            )

            def mix():
                for n in range(0, cur.shape[1], WIDE):
                    mix_block(64, cur, r["mixed"], r["w"], n, (own, r["w_other"]))

            if t == STEPS - 1:
                pl.when(layer == 0)(mix)
            else:
                mix()
            add_stats(r["stats"], 2 * layer, sums, counts)
            return carry

        lax.fori_loop(0, 2, one, 0)


def stats_table(r):
    table = jnp.transpose(
        jnp.concatenate([r["stats"][...], jnp.zeros((128 - 60, 128), jnp.float32)], axis=0)
    )
    for layer in range(2):
        row = table[2 * layer : 2 * layer + 1, :]
        counts = table[2 * layer + 1 : 2 * layer + 2, :]
        at = lax.broadcasted_iota(jnp.int32, row.shape, 1)
        row = jnp.where(at < 60, row, jnp.where(at >= 64, pltpu.roll(counts, 64, 1), 0.0))
        r["table"][32 * layer : 32 * layer + 32, :] = jnp.broadcast_to(row, (32, 128))


def step_kernel(t, names, *refs):
    r = dict(zip(names, refs))
    chip, core = lax.axis_index("x"), lax.axis_index("c")
    first, second = (chip == 0) & (core == 0), (chip == 0) & (core == 1)
    if "stats_in" in r:
        r["stats"][...] = r["stats_in"][...]
    else:
        r["stats"][...] = jnp.zeros_like(r["stats"])
    if t == 0:
        first_step(r, first, second)
    elif t < LAST_RELAY:
        relay_step(t, r | {"w": r["w_relay"]}, first, second, core)
    if t >= FIRST_PAIR:
        pair_step(t, r, chip, core)
    if t == STEPS - 1:
        stats_table(r)


def tail_kernel(names, *refs):
    r = dict(zip(names, refs))
    chip, core = lax.axis_index("x"), lax.axis_index("c")
    for k in range(CHIPS - 1):

        @pl.when(chip == k)
        def _():
            pltpu.make_async_copy(r[f"part{k}"], r["out"], r["sem"]).start()

    blocks = list(enumerate(range(0, r["cur"].shape[1], WIDE)))
    for own, source in ((True, r["w_hbm"]), (False, r["w_other_hbm"])):

        @pl.when((chip == CHIPS - 1) & ((core == 1) if own else (core == 0)))
        def _():
            for i, n in blocks:
                weight_copy({"w_hbm": source, "w": r["w"]}, r["wsem"], i, n).start()

    @pl.when(chip == CHIPS - 1)
    def _():
        r["cur"][...] = r["mid"][...]
        for i, n in blocks:
            weight_copy({"w_hbm": r["w_hbm"], "w": r["w"]}, r["wsem"], i, n).wait()
            mix_block(64, r["cur"], r["mixed"], r["w"], n)
        pltpu.make_async_copy(r["cur"], r["out"], r["sem"]).start()

    pltpu.make_async_copy(r["cur"], r["out"], r["sem"]).wait()


def loss_kernel(token_total, arrived, balance):
    total = jnp.sum(arrived[...], axis=0, keepdims=True)
    counts = pltpu.roll(total, 64, 1)
    at = lax.broadcasted_iota(jnp.int32, total.shape, 1)
    terms = jnp.where(at < 60, (counts / (token_total * 4.0)) * (total / token_total), 0.0)
    balance[0] = 60.0 * jnp.sum(terms)


def call(kernel, ins, outs, scratch, flops):
    names_in, names_out = tuple(ins), tuple(outs)
    space = {n: pltpu.HBM if n.endswith("_hbm") or n == "hidden" else pltpu.VMEM for n in ins}
    args = [pltpu.with_memory_space_constraint(ins[n], space[n]) for n in names_in]
    place = {"out": pltpu.HBM, "balance": pltpu.SMEM}
    out_space = {n: place.get(n, pltpu.VMEM) for n in outs}
    got = pl.pallas_call(
        kernel,
        out_shape=[out_space[n](*outs[n]) for n in names_out],
        in_specs=[pl.BlockSpec(memory_space=space[n]) for n in names_in],
        out_specs=[pl.BlockSpec(memory_space=out_space[n]) for n in names_out],
        scratch_shapes=list(scratch.values()),
        compiler_params=pltpu.CompilerParams(vmem_limit_bytes=VMEM_LIMIT),
        cost_estimate=pl.CostEstimate(
            flops=flops, bytes_accessed=8 * 1024 * 1024, transcendentals=0
        ),
    )(*args)
    return dict(zip(names_out, got))


def run_step(t, ins, outs):
    rows = 128 if 2 <= t < LAST_RELAY else 64
    scratch = {
        "nrm": pltpu.VMEM((rows, 2048), jnp.float32),
        "nbf": pltpu.VMEM((rows, 2048), jnp.bfloat16),
    }
    if "mixed" not in outs:
        scratch["mixed"] = pltpu.VMEM((rows, 2048), jnp.bfloat16)
    if 4 <= t < LAST_RELAY:
        scratch["cur"] = pltpu.VMEM((128, 2048), jnp.bfloat16)
    if t < 5:
        scratch["xsem"] = pltpu.SemaphoreType.DMA((2,))
    if "stats" not in outs:
        scratch["stats"] = pltpu.VMEM((60, 128), jnp.float32)
    if t == 0:
        scratch["wsem"] = pltpu.SemaphoreType.DMA((4,))
        scratch["ssem"] = pltpu.SemaphoreType.DMA((4,))
    kernel = functools.partial(step_kernel, t, (*ins, *outs, *scratch))
    return call(kernel, ins, outs, scratch, 2 * 64 * 2048 * 2048 * 2)


def hop_pairs(t):
    pairs = [(1, 3)] if 3 <= t < LAST_RELAY else []
    for chip in (1, 2, 3):
        chunk = t - 3 - 2 * chip
        if 0 <= chunk < CHUNKS:
            goal = chip + 1 if chip < CHIPS - 1 else chunk
            pairs += [(2 * chip + c, 2 * goal + c) for c in range(2)]
    return pairs


def per_device(hidden_in, norm_gain, router_weight, expert_scale, mix_weight, routes):
    batches, rows, width = hidden_in.shape
    experts = router_weight.shape[2]
    router = jnp.transpose(router_weight[0])
    ids = jnp.transpose(routes[0], (0, 2, 1))
    scale, w = expert_scale[0], mix_weight[0]
    swap = [(2 * x + c, 2 * x + 1 - c) for x in range(1, CHIPS) for c in range(2)]

    def hop(x, pairs):
        return lax.ppermute(x, SEC, pairs)

    half = ((rows, width), jnp.bfloat16)
    full = ((2 * rows, width), jnp.bfloat16)
    stats_shape = ((experts, 128), jnp.float32)
    own = {"w": w, "router": router, "scale": scale, "gain": norm_gain, "ids": ids}
    w_other = hop(w, swap)
    got = run_step(
        0,
        {"hidden": hidden_in, **{n + "_hbm": v for n, v in own.items()}},
        {
            **{n: (v.shape, v.dtype) for n, v in own.items()},
            "sendR": half,
            "stats": stats_shape,
            "small": ((176, width), jnp.bfloat16),
        },
    )
    small, stats = got["small"], got["stats"]
    relay = {("w_relay" if n == "w" else n): got[n] for n in own}
    recv = {("R", 0): hop(got["sendR"], [(0, 1)])}
    for t in range(1, STEPS):
        ins, outs = {"stats_in": stats}, {"stats": stats_shape}
        if t < LAST_RELAY:
            ins |= relay
        if t < 5:
            ins["hidden"] = hidden_in
            outs["sendR"] = half if t == 1 else full
        if 2 <= t < LAST_RELAY:
            ins["recvR"] = recv[("R", t - 2)]
        if t in (2, 4, 5, 6):
            outs["sendA"] = half
        if t >= 3:
            outs["sendB"] = half
        if t >= FIRST_PAIR:
            ins |= {"small": small, "small_other": small_other, "w": w, "w_other": w_other}
            ins["recvB"] = recv[("B", t - 2)]
            at = 2 if t == FIRST_PAIR else t - 2
            if ("A", at) in recv:
                ins["recvA"] = recv[("A", at)]
        if t == STEPS - 1:
            outs = {"sendB": half, "mixed": half, "table": ((2 * 32, 128), jnp.float32)}
        got = run_step(t, ins, outs)
        stats = got.get("stats")
        if "sendA" in got:
            recv[("A", t)] = hop(got["sendA"], [(1, 2)])
        if t < STEPS - 1 and "sendB" in got:
            recv[("B", t)] = hop(got["sendB"], hop_pairs(t))
        if "sendR" in got:
            recv[("R", t)] = hop(got["sendR"], [(0, 1)])
        if t == 2:
            small_other = hop(small, swap)
    arrived = lax.all_to_all(got["table"], ("c", "z", "y"), 0, 0, tiled=True)
    ins = {f"part{k}": recv[("B", k + 9)] for k in range(CHUNKS - 1)}
    ins |= {"mid": got["sendB"], "mixed": got["mixed"], "w_hbm": w, "w_other_hbm": w_other}
    scratch = {"cur": pltpu.VMEM(*half), "w": pltpu.VMEM(w.shape, w.dtype)}
    scratch |= {"sem": pltpu.SemaphoreType.DMA, "wsem": pltpu.SemaphoreType.DMA((4,))}
    kernel = functools.partial(tail_kernel, (*ins, "out", *scratch))
    out = call(kernel, ins, {"out": half}, scratch, 2 * 64 * 2048 * 2048)["out"]
    token_total = float(batches * rows * lax.axis_size("z") * lax.axis_size("y"))
    kernel = functools.partial(loss_kernel, token_total)
    loss = call(kernel, {"arrived": arrived}, {"balance": ((1,), jnp.float32)}, {}, 1000)
    return out[None], loss["balance"]


def solution(mesh):
    torus = Mesh(mesh.devices.reshape(CHIPS, 2, 8, 4), ("x", "c", "z", "y"))
    dp = ("z", "y")

    return jax.shard_map(
        per_device,
        mesh=torus,
        in_specs=(
            P(None, dp, None),
            P(SEC, None),
            P(SEC, None, None),
            P(SEC, None, None),
            P(SEC, None, None),
            P(SEC, None, dp, None),
        ),
        out_specs=(P(SEC, dp, None), P(SEC)),
        check_vma=False,
    )
```

time: 97 us -> 109 us (1.12)
  waiting for transfers between devices: 24.9 us -> 40.4 us
  blocking collectives: 23.8 us -> 21.4 us
  starting transfers between devices: 23 us -> 21.6 us
    ppermute x20, waiting for transfers between devices: 24.9 us -> 40.4 us  [hop(): return lax.ppermute(x, SEC, pairs)]
    all_to_all x1, blocking collectives: 23.8 us -> 21.4 us  [per_device(): arrived = lax.all_to_all(got['table'], ('c', 'z', 'y'), 0, 0, tiled=True)]
    ppermute x20, starting transfers between devices: 23 us -> 21.6 us  [hop(): return lax.ppermute(x, SEC, pairs)]
    pallas_call x13 -> x15, Pallas kernels: 23 us -> 23.3 us  [call(): pl.pallas_call(kernel, out_shape=[out_space[n](*outs[n]) for n in names_o...]
  transfers between devices with their start and end apart: 20 -> 20, of which waited for: 4 -> 4; matrix products, arithmetic and copies ran while one was open for 0% -> 0% of each run, Pallas kernels for 23% -> 17%
where the time goes in v1:
time: 109 us; the launch traced here: 108 us
  waiting for transfers between devices  40.4 us (37%)
  Pallas kernels  23.3 us (21%)
  starting transfers between devices  21.6 us (20%)
  blocking collectives  21.4 us (20%)
  between operations  1.77 us (2%)
    ppermute x20, waiting for transfers between devices, hop(): return lax.ppermute(x, SEC, pairs)  40.4 us
    pallas_call x15, Pallas kernels, call(): pl.pallas_call(kernel, out_shape=[out_space[n](*outs[n]) for n in names_o...  23.3 us
    ppermute x20, starting transfers between devices, hop(): return lax.ppermute(x, SEC, pairs)  21.6 us
    all_to_all x1, blocking collectives, per_device(): arrived = lax.all_to_all(got['table'], ('c', 'z', 'y'), 0, 0, tiled=True)  21.4 us
  transfers between devices with their start and end apart: 20, of which 4 were waited for; matrix products, arithmetic and copies ran while one was open for 0% of the time, Pallas kernels for 17%

profile of v1, /device:TPU:7, one launch (start us, length us, event | category | flops | bytes accessed | tf_op | source)
XLA Modules:
  0.0 108.5 jit_solution(1097355893544138148)
XLA Ops:
  0.6 2.6 %collective-permute-start.5 = (bf16[2048,2048]{1,0:T(8,128)(2,1)}, bf16[2048,2048]{1,0:T(8,128)(2,1)S(1)}, u32[]{:S(2)}, u32[]{:S(2)}) collective-permute-start(bf16[2048,2048]{1,0:T(8,128)(2,1)} %bitcast.13), channel_id=1, source_target_pairs={{64,96},{96,64},{128,160},{160,128},{192,224},{224,192},{65,97},{9... | collective-permute-start | bytes 25165832 | tf_op jit(solution)/shard_map/ppermute | solution.py:417
  3.2 1.2 %shard_map.77 = (bf16[2048,2048]{1,0:T(8,128)(2,1)S(1)}, bf16[60,2048]{1,0:T(8,128)(2,1)S(1)}, bf16[60,2048]{1,0:T(8,128)(2,1)S(1)}, bf16[1,2048]{1,0:T(2,128)(2...) custom-call(bf16[8,64,2048]{2,1,0:T(8,128)(2,1)} %refs_6_.7, ...), custom_call_target="tpu_custom_call" | custom-call | flops 1073741824 | bytes 8388608 | tf_op jit(solution)/shard_map/pallas_call | solution.py:363
  4.4 0.7 collective-permute-start
  5.2 0.0 collective-permute-done.refs_7_
  5.2 0.7 collective-permute-start.2
  5.9 0.7 collective-permute-start.1
  6.6 1.9 %collective-permute-start.4 = (bf16[176,2048]{1,0:T(8,128)(2,1)S(1)}, bf16[176,2048]{1,0:T(8,128)(2,1)S(1)}, u32[]{:S(2)}, u32[]{:S(2)}) collective-permute-start(bf16[176,2048]{1,0:T(8,128)(2,1)S(1)} %get-tuple-element.55.refs_7_.refs_1_), channel_id=1, source_target_pairs={{64,96},{96,64},{128,160},{160,128},{192,224},{224,192},{65,97},{9... | collective-permute-start | bytes 2162696 | tf_op jit(solution)/shard_map/ppermute | solution.py:417
  8.5 0.7 collective-permute-start.7
  9.2 0.0 collective-permute-done.1.refs_7_
  9.2 0.0 slice-start
  9.3 0.8 collective-permute-start.3
  10.1 0.0 collective-permute-done.2.refs_7_
  10.1 0.8 collective-permute-start.6
  11.0 0.0 slice-start.1
  11.0 0.1 shard_map.81
  11.0 0.0 collective-permute-done.7.refs_12_
  11.0 0.8 collective-permute-start.8
  11.9 0.0 collective-permute-done.6.refs_11_
  11.9 0.8 collective-permute-start.9
  12.7 4.5 %collective-permute-done.4.refs_8_.refs_2_ = bf16[176,2048]{1,0:T(8,128)(2,1)S(1)} collective-permute-done((bf16[176,2048]{1,0:T(8,128)(2,1)S(1)}, bf16[176,2048]{1,0:T(8,128)(2,1)S(1)}, u32[]{:S(2)}, u32[]{:S(2)}) %collective-permute-start.4) | collective-permute-done | bytes 720928 | tf_op jit(solution)/shard_map/ppermute | solution.py:417
  17.2 0.7 collective-permute-start.10
  17.9 0.0 collective-permute-done.3.refs_6_
  17.9 0.0 collective-permute-done.5.refs_10_.refs_4_.refs_6_
  17.9 0.0 copy-start
  17.9 0.0 slice-done
  17.9 0.0 slice-done.1
  18.0 0.2 shard_map.82
  18.2 0.7 collective-permute-start.11
  18.9 0.7 collective-permute-start.12
  19.5 0.0 collective-permute-done.9.refs_11_
  19.6 0.0 collective-permute-done.10.refs_12_
  19.6 0.0 collective-permute-done.8.refs_6_
  19.6 0.7 collective-permute-start.13
  20.3 0.7 collective-permute-start.14
  21.0 0.0 collective-permute-done.11.refs_5_
  21.0 0.0 collective-permute-done.12.refs_6_
  21.0 1.3 %collective-permute-start.15 = (bf16[64,2048]{1,0:T(8,128)(2,1)S(1)}, bf16[64,2048]{1,0:T(8,128)(2,1)S(1)}, u32[]{:S(2)}, u32[]{:S(2)}) collective-permute-start(bf16[64,2048]{1,0:T(8,128)(2,1)S(1)} %get-tuple-element.69), channel_id=1, source_target_pairs={{64,128},{96,160},{128,192},{160,224},{65,129},{97,161},{129,193},... | collective-permute-start | bytes 786440 | tf_op jit(solution)/shard_map/ppermute | solution.py:417
  22.3 0.0 collective-permute-done.13.refs_5_
  22.3 0.0 collective-permute-done.14.refs_6_
  22.4 1.3 %collective-permute-start.17 = (bf16[64,2048]{1,0:T(8,128)(2,1)S(1)}, bf16[64,2048]{1,0:T(8,128)(2,1)S(1)}, u32[]{:S(2)}, u32[]{:S(2)}) collective-permute-start(bf16[64,2048]{1,0:T(8,128)(2,1)S(1)} %get-tuple-element.72), channel_id=1, source_target_pairs={{64,128},{96,160},{128,192},{160,224},{65,129},{97,161},{129,193},... | collective-permute-start | bytes 786440 | tf_op jit(solution)/shard_map/ppermute | solution.py:417
  23.7 30.2 %collective-permute-done.15.refs_5_ = bf16[64,2048]{1,0:T(8,128)(2,1)S(1)} collective-permute-done((bf16[64,2048]{1,0:T(8,128)(2,1)S(1)}, bf16[64,2048]{1,0:T(8,128)(2,1)S(1)}, u32[]{:S(2)}, u32[]{:S(2)}) %collective-permute-start.15) | collective-permute-done | bytes 262176 | tf_op jit(solution)/shard_map/ppermute | solution.py:417
  53.9 4.4 %shard_map.86 = (f32[60,128]{1,0:T(8,128)S(1)}, bf16[64,2048]{1,0:T(8,128)(2,1)S(1)}) custom-call(f32[60,128]{1,0:T(8,128)S(1)} %get-tuple-element.68.refs_0_, bf16[176,2048]{1,0:T(8,128)(2,1)S(1)} %get-tuple-element.55.refs_7_.refs_1_, bf16[176,2048]{1,0:T(8,128)(2,1)S(1)} %collective-permute-done.4.refs_8_.refs_2_, bf16[2048,2048]{1,0:T(8,128)(2,1)S(1)} %bitcast.22, ...), custom_call_target="tpu_custom_call" | custom-call | flops 1073741824 | bytes 8388608 | tf_op jit(solution)/shard_map/pallas_call | solution.py:363
  58.3 1.9 %collective-permute-start.16 = (bf16[64,2048]{1,0:T(8,128)(2,1)S(1)}, bf16[64,2048]{1,0:T(8,128)(2,1)S(1)}, u32[]{:S(2)}, u32[]{:S(2)}) collective-permute-start(bf16[64,2048]{1,0:T(8,128)(2,1)S(1)} %get-tuple-element.70), channel_id=1, source_target_pairs={{128,192},{160,224},{192,0},{224,32},{129,193},{161,225},{193,1},{... | collective-permute-start | bytes 786440 | tf_op jit(solution)/shard_map/ppermute | solution.py:417
  60.3 5.2 %collective-permute-done.17.refs_5_ = bf16[64,2048]{1,0:T(8,128)(2,1)S(1)} collective-permute-done((bf16[64,2048]{1,0:T(8,128)(2,1)S(1)}, bf16[64,2048]{1,0:T(8,128)(2,1)S(1)}, u32[]{:S(2)}, u32[]{:S(2)}) %collective-permute-start.17) | collective-permute-done | bytes 262176 | tf_op jit(solution)/shard_map/ppermute | solution.py:417
  65.5 4.4 %shard_map.87 = (f32[60,128]{1,0:T(8,128)S(1)}, bf16[64,2048]{1,0:T(8,128)(2,1)S(1)}) custom-call(f32[60,128]{1,0:T(8,128)S(1)} %get-tuple-element.71.refs_0_, bf16[176,2048]{1,0:T(8,128)(2,1)S(1)} %get-tuple-element.55.refs_7_.refs_1_, bf16[176,2048]{1,0:T(8,128)(2,1)S(1)} %collective-permute-done.4.refs_8_.refs_2_, bf16[2048,2048]{1,0:T(8,128)(2,1)S(1)} %bitcast.23, ...), custom_call_target="tpu_custom_call" | custom-call | flops 1073741824 | bytes 8388608 | tf_op jit(solution)/shard_map/pallas_call | solution.py:363
  69.9 1.9 %collective-permute-start.18 = (bf16[64,2048]{1,0:T(8,128)(2,1)S(1)}, bf16[64,2048]{1,0:T(8,128)(2,1)S(1)}, u32[]{:S(2)}, u32[]{:S(2)}) collective-permute-start(bf16[64,2048]{1,0:T(8,128)(2,1)S(1)} %get-tuple-element.73), channel_id=1, source_target_pairs={{128,192},{160,224},{192,64},{224,96},{129,193},{161,225},{193,65}... | collective-permute-start | bytes 786440 | tf_op jit(solution)/shard_map/ppermute | solution.py:417
  71.8 0.0 collective-permute-done.16.refs_5_.refs_0_
  71.9 4.5 %shard_map.88 = (f32[60,128]{1,0:T(8,128)S(1)}, bf16[64,2048]{1,0:T(8,128)(2,1)S(1)}) custom-call(f32[60,128]{1,0:T(8,128)S(1)} %get-tuple-element.74.refs_0_, bf16[176,2048]{1,0:T(8,128)(2,1)S(1)} %get-tuple-element.55.refs_7_.refs_1_, bf16[176,2048]{1,0:T(8,128)(2,1)S(1)} %collective-permute-done.4.refs_8_.refs_2_, bf16[2048,2048]{1,0:T(8,128)(2,1)S(1)} %bitcast.24, ...), custom_call_target="tpu_custom_call" | custom-call | flops 1073741824 | bytes 8388608 | tf_op jit(solution)/shard_map/pallas_call | solution.py:363
  76.3 1.3 %collective-permute-start.19 = (bf16[64,2048]{1,0:T(8,128)(2,1)S(1)}, bf16[64,2048]{1,0:T(8,128)(2,1)S(1)}, u32[]{:S(2)}, u32[]{:S(2)}) collective-permute-start(bf16[64,2048]{1,0:T(8,128)(2,1)S(1)} %get-tuple-element.75), channel_id=1, source_target_pairs={{192,128},{224,160},{193,129},{225,161},{194,130},{226,162},{195,1... | collective-permute-start | bytes 786440 | tf_op jit(solution)/shard_map/ppermute | solution.py:417
  77.7 0.4 collective-permute-done.18.refs_5_.refs_1_
  78.1 0.0 copy-done
  78.1 3.3 %shard_map.89 = (bf16[64,2048]{1,0:T(8,128)(2,1)S(1)}, bf16[64,2048]{1,0:T(8,128)(2,1)S(1)}, f32[64,128]{1,0:T(8,128)S(1)}) custom-call(f32[60,128]{1,0:T(8,128)S(1)} %get-tuple-element.76.refs_0_, bf16[176,2048]{1,0:T(8,128)(2,1)S(1)} %get-tuple-element.55.refs_7_.refs_1_, bf16[176,2048]{1,0:T(8,128)(2,1)S(1)} %collective-permute-done.4.refs_8_.refs_2_, ...), custom_call_target="tpu_custom_call" | custom-call | flops 1073741824 | bytes 8388608 | tf_op jit(solution)/shard_map/pallas_call | solution.py:363
  81.4 21.4 %all_to_all.11 = f32[64,1,128]{2,1,0:T(1,128)S(1)} all-to-all(f32[64,1,128]{2,1,0:T(1,128)S(1)} %bitcast.27), channel_id=1, replica_groups=mesh['x'=4,'c'=2,'z'=8,'y'=4] {'c','z','y'}, dimensions={0} | all-to-all | bytes 65536 | tf_op jit(solution)/shard_map/all_to_all | solution.py:468
  102.8 0.2 shard_map.91
  103.5 0.0 collective-permute-done.19.refs_2_
  103.5 4.8 %shard_map.90 = bf16[64,2048]{1,0:T(8,128)(2,1)} custom-call(bf16[64,2048]{1,0:T(8,128)(2,1)S(1)} %collective-permute-done.16.refs_5_.refs_0_, bf16[64,2048]{1,0:T(8,128)(2,1)S(1)} %collective-permute-done.18.refs_5_.refs_1_, bf16[64,2048]{1,0:T(8,128)(2,1)S(1)} %collective-permute-done.19.refs_2_, bf16[64,2048]{1,0:T(8,128)(2,1)S(1)} %get-tuple-element.77.refs_3_, ...), custom_call_target="tpu_custom_call" | custom-call | flops 536870912 | bytes 8388608 | tf_op jit(solution)/shard_map/pallas_call | solution.py:363
  (7 shorter events, 0.2 us)
Async XLA Ops:
  0.6 17.3 %collective-permute-start.5 = (bf16[2048,2048]{1,0:T(8,128)(2,1)}, bf16[2048,2048]{1,0:T(8,128)(2,1)S(1)}, u32[]{:S(2)}, u32[]{:S(2)}) collective-permute-start(bf16[2048,2048]{1,0:T(8,128)(2,1)} %bitcast.13), channel_id=1, source_target_pairs={{64,96},{96,64},{128,160},{160,128},{192,224},{224,192},{65,97},{9... | collective-permute-start | bytes 25165832 | tf_op jit(solution)/shard_map/ppermute | solution.py:417
  4.4 0.7 collective-permute-start
  5.2 4.9 %collective-permute-start.2 = (bf16[128,2048]{1,0:T(8,128)(2,1)S(1)}, bf16[128,2048]{1,0:T(8,128)(2,1)S(1)}, u32[]{:S(2)}, u32[]{:S(2)}) collective-permute-start(bf16[128,2048]{1,0:T(8,128)(2,1)S(1)} %get-tuple-element.52), channel_id=1, source_target_pairs={{0,32},{1,33},{2,34},{3,35},{4,36},{5,37},{6,38},{7,39},{8,40},{9,... | collective-permute-start | bytes 1572872 | tf_op jit(solution)/shard_map/ppermute | solution.py:417
  5.9 3.3 %collective-permute-start.1 = (bf16[64,2048]{1,0:T(8,128)(2,1)S(1)}, bf16[64,2048]{1,0:T(8,128)(2,1)S(1)}, u32[]{:S(2)}, u32[]{:S(2)}) collective-permute-start(bf16[64,2048]{1,0:T(8,128)(2,1)S(1)} %get-tuple-element.50), channel_id=1, source_target_pairs={{0,32},{1,33},{2,34},{3,35},{4,36},{5,37},{6,38},{7,39},{8,40},{9,... | collective-permute-start | bytes 786440 | tf_op jit(solution)/shard_map/ppermute | solution.py:417
  6.6 10.6 %collective-permute-start.4 = (bf16[176,2048]{1,0:T(8,128)(2,1)S(1)}, bf16[176,2048]{1,0:T(8,128)(2,1)S(1)}, u32[]{:S(2)}, u32[]{:S(2)}) collective-permute-start(bf16[176,2048]{1,0:T(8,128)(2,1)S(1)} %get-tuple-element.55.refs_7_.refs_1_), channel_id=1, source_target_pairs={{64,96},{96,64},{128,160},{160,128},{192,224},{224,192},{65,97},{9... | collective-permute-start | bytes 2162696 | tf_op jit(solution)/shard_map/ppermute | solution.py:417
  8.5 2.5 %collective-permute-start.7 = (bf16[64,2048]{1,0:T(8,128)(2,1)S(1)}, bf16[64,2048]{1,0:T(8,128)(2,1)S(1)}, u32[]{:S(2)}, u32[]{:S(2)}) collective-permute-start(bf16[64,2048]{1,0:T(8,128)(2,1)S(1)} %get-tuple-element.57), channel_id=1, source_target_pairs={{32,64},{33,65},{34,66},{35,67},{36,68},{37,69},{38,70},{39,71},{4... | collective-permute-start | bytes 786440 | tf_op jit(solution)/shard_map/ppermute | solution.py:417
  9.2 8.7 %slice-start = ((s8[8388608]{0:T(1024)(128)(4,1)}), s8[4194304]{0:T(1024)(128)(4,1)S(1)}, s32[]{:S(2)}) async-start(s8[8388608]{0:T(1024)(128)(4,1)} %bitcast.16), calls=%async_computation.1 | async-start | bytes 8388608
  9.3 8.6 %collective-permute-start.3 = (bf16[128,2048]{1,0:T(8,128)(2,1)S(1)}, bf16[128,2048]{1,0:T(8,128)(2,1)S(1)}, u32[]{:S(2)}, u32[]{:S(2)}) collective-permute-start(bf16[128,2048]{1,0:T(8,128)(2,1)S(1)} %get-tuple-element.54), channel_id=1, source_target_pairs={{0,32},{1,33},{2,34},{3,35},{4,36},{5,37},{6,38},{7,39},{8,40},{9,... | collective-permute-start | bytes 1572872 | tf_op jit(solution)/shard_map/ppermute | solution.py:417
  10.1 1.7 %collective-permute-start.6 = (bf16[64,2048]{1,0:T(8,128)(2,1)S(1)}, bf16[64,2048]{1,0:T(8,128)(2,1)S(1)}, u32[]{:S(2)}, u32[]{:S(2)}) collective-permute-start(bf16[64,2048]{1,0:T(8,128)(2,1)S(1)} %get-tuple-element.56), channel_id=1, source_target_pairs={{32,96},{33,97},{34,98},{35,99},{36,100},{37,101},{38,102},{39,103... | collective-permute-start | bytes 786440 | tf_op jit(solution)/shard_map/ppermute | solution.py:417
  11.0 7.0 %slice-start.1 = ((s8[8388608]{0:T(1024)(128)(4,1)}), s8[4194304]{0:T(1024)(128)(4,1)S(1)}, s32[]{:S(2)}) async-start(s8[8388608]{0:T(1024)(128)(4,1)} %bitcast.16), calls=%async_computation.2 | async-start | bytes 8388608
  11.0 8.5 %collective-permute-start.8 = (bf16[128,2048]{1,0:T(8,128)(2,1)S(1)}, bf16[128,2048]{1,0:T(8,128)(2,1)S(1)}, u32[]{:S(2)}, u32[]{:S(2)}) collective-permute-start(bf16[128,2048]{1,0:T(8,128)(2,1)S(1)} %get-tuple-element.59), channel_id=1, source_target_pairs={{0,32},{1,33},{2,34},{3,35},{4,36},{5,37},{6,38},{7,39},{8,40},{9,... | collective-permute-start | bytes 1572872 | tf_op jit(solution)/shard_map/ppermute | solution.py:417
  11.9 7.7 %collective-permute-start.9 = (bf16[64,2048]{1,0:T(8,128)(2,1)S(1)}, bf16[64,2048]{1,0:T(8,128)(2,1)S(1)}, u32[]{:S(2)}, u32[]{:S(2)}) collective-permute-start(bf16[64,2048]{1,0:T(8,128)(2,1)S(1)} %get-tuple-element.60), channel_id=1, source_target_pairs={{32,96},{33,97},{34,98},{35,99},{36,100},{37,101},{38,102},{39,103... | collective-permute-start | bytes 786440 | tf_op jit(solution)/shard_map/ppermute | solution.py:417
  17.2 2.3 %collective-permute-start.10 = (bf16[64,2048]{1,0:T(8,128)(2,1)S(1)}, bf16[64,2048]{1,0:T(8,128)(2,1)S(1)}, u32[]{:S(2)}, u32[]{:S(2)}) collective-permute-start(bf16[64,2048]{1,0:T(8,128)(2,1)S(1)} %get-tuple-element.61), channel_id=1, source_target_pairs={{32,64},{33,65},{34,66},{35,67},{36,68},{37,69},{38,70},{39,71},{4... | collective-permute-start | bytes 786440 | tf_op jit(solution)/shard_map/ppermute | solution.py:417
  17.9 60.1 %copy-start = (bf16[2048,2048]{1,0:T(8,128)(2,1)}, bf16[2048,2048]{1,0:T(8,128)(2,1)S(1)}, u32[]{:S(2)}) copy-start(bf16[2048,2048]{1,0:T(8,128)(2,1)S(1)} %collective-permute-done.5.refs_10_.refs_4_.refs_6_) | copy-start | bytes 25165828
  18.2 2.8 %collective-permute-start.11 = (bf16[64,2048]{1,0:T(8,128)(2,1)S(1)}, bf16[64,2048]{1,0:T(8,128)(2,1)S(1)}, u32[]{:S(2)}, u32[]{:S(2)}) collective-permute-start(bf16[64,2048]{1,0:T(8,128)(2,1)S(1)} %get-tuple-element.63), channel_id=1, source_target_pairs={{32,96},{64,128},{96,160},{33,97},{65,129},{97,161},{34,98},{66,13... | collective-permute-start | bytes 786440 | tf_op jit(solution)/shard_map/ppermute | solution.py:417
  18.9 2.1 %collective-permute-start.12 = (bf16[64,2048]{1,0:T(8,128)(2,1)S(1)}, bf16[64,2048]{1,0:T(8,128)(2,1)S(1)}, u32[]{:S(2)}, u32[]{:S(2)}) collective-permute-start(bf16[64,2048]{1,0:T(8,128)(2,1)S(1)} %get-tuple-element.64), channel_id=1, source_target_pairs={{32,64},{33,65},{34,66},{35,67},{36,68},{37,69},{38,70},{39,71},{4... | collective-permute-start | bytes 786440 | tf_op jit(solution)/shard_map/ppermute | solution.py:417
  19.6 2.7 %collective-permute-start.13 = (bf16[64,2048]{1,0:T(8,128)(2,1)S(1)}, bf16[64,2048]{1,0:T(8,128)(2,1)S(1)}, u32[]{:S(2)}, u32[]{:S(2)}) collective-permute-start(bf16[64,2048]{1,0:T(8,128)(2,1)S(1)} %get-tuple-element.66), channel_id=1, source_target_pairs={{32,96},{64,128},{96,160},{33,97},{65,129},{97,161},{34,98},{66,13... | collective-permute-start | bytes 786440 | tf_op jit(solution)/shard_map/ppermute | solution.py:417
  20.3 2.0 %collective-permute-start.14 = (bf16[64,2048]{1,0:T(8,128)(2,1)S(1)}, bf16[64,2048]{1,0:T(8,128)(2,1)S(1)}, u32[]{:S(2)}, u32[]{:S(2)}) collective-permute-start(bf16[64,2048]{1,0:T(8,128)(2,1)S(1)} %get-tuple-element.67), channel_id=1, source_target_pairs={{32,64},{33,65},{34,66},{35,67},{36,68},{37,69},{38,70},{39,71},{4... | collective-permute-start | bytes 786440 | tf_op jit(solution)/shard_map/ppermute | solution.py:417
  21.0 32.8 %collective-permute-start.15 = (bf16[64,2048]{1,0:T(8,128)(2,1)S(1)}, bf16[64,2048]{1,0:T(8,128)(2,1)S(1)}, u32[]{:S(2)}, u32[]{:S(2)}) collective-permute-start(bf16[64,2048]{1,0:T(8,128)(2,1)S(1)} %get-tuple-element.69), channel_id=1, source_target_pairs={{64,128},{96,160},{128,192},{160,224},{65,129},{97,161},{129,193},... | collective-permute-start | bytes 786440 | tf_op jit(solution)/shard_map/ppermute | solution.py:417
  22.4 43.1 %collective-permute-start.17 = (bf16[64,2048]{1,0:T(8,128)(2,1)S(1)}, bf16[64,2048]{1,0:T(8,128)(2,1)S(1)}, u32[]{:S(2)}, u32[]{:S(2)}) collective-permute-start(bf16[64,2048]{1,0:T(8,128)(2,1)S(1)} %get-tuple-element.72), channel_id=1, source_target_pairs={{64,128},{96,160},{128,192},{160,224},{65,129},{97,161},{129,193},... | collective-permute-start | bytes 786440 | tf_op jit(solution)/shard_map/ppermute | solution.py:417
  58.3 13.5 %collective-permute-start.16 = (bf16[64,2048]{1,0:T(8,128)(2,1)S(1)}, bf16[64,2048]{1,0:T(8,128)(2,1)S(1)}, u32[]{:S(2)}, u32[]{:S(2)}) collective-permute-start(bf16[64,2048]{1,0:T(8,128)(2,1)S(1)} %get-tuple-element.70), channel_id=1, source_target_pairs={{128,192},{160,224},{192,0},{224,32},{129,193},{161,225},{193,1},{... | collective-permute-start | bytes 786440 | tf_op jit(solution)/shard_map/ppermute | solution.py:417
  69.9 8.1 %collective-permute-start.18 = (bf16[64,2048]{1,0:T(8,128)(2,1)S(1)}, bf16[64,2048]{1,0:T(8,128)(2,1)S(1)}, u32[]{:S(2)}, u32[]{:S(2)}) collective-permute-start(bf16[64,2048]{1,0:T(8,128)(2,1)S(1)} %get-tuple-element.73), channel_id=1, source_target_pairs={{128,192},{160,224},{192,64},{224,96},{129,193},{161,225},{193,65}... | collective-permute-start | bytes 786440 | tf_op jit(solution)/shard_map/ppermute | solution.py:417
  76.3 27.2 %collective-permute-start.19 = (bf16[64,2048]{1,0:T(8,128)(2,1)S(1)}, bf16[64,2048]{1,0:T(8,128)(2,1)S(1)}, u32[]{:S(2)}, u32[]{:S(2)}) collective-permute-start(bf16[64,2048]{1,0:T(8,128)(2,1)S(1)} %get-tuple-element.75), channel_id=1, source_target_pairs={{192,128},{224,160},{193,129},{225,161},{194,130},{226,162},{195,1... | collective-permute-start | bytes 786440 | tf_op jit(solution)/shard_map/ppermute | solution.py:417
